TPU v7x, 32 devices: a whole 2x2x4 slice. The times are simulated.
32 devices in a mesh: dp: 16 (over z, y, core), tensor: 2 (over x).
Axes of the slice: x: 2, y: 2, z: 4, core: 2. Of those that a mesh axis runs over, the one named last changes fastest.
Arguments:
- activations: bfloat16 [4096, 27648], P('dp', 'tensor'), may hold values from -6 to 6
- output_gradient: bfloat16 [4096, 5120], P('dp', 'tensor'), may hold values from -6 to 6
- adapter_a: bfloat16 [2, 13824, 128], P('tensor', 'dp'), may hold values from -0.0390625 to 0.0390625
- adapter_b: bfloat16 [128, 5120], P(None, 'tensor'), may hold values from -0.078125 to 0.078125
- log_ratio: float32 [4096], P('dp'), may hold values from -1.5 to 1.5
- lengths: int32 [1, 16], replicated, may hold values from 1 to 256, as said below
- rewards: int32 [1, 16], replicated, may hold values from 0 to 10
Outputs:
- grad_a: float32 [2, 13824, 128], P('tensor', 'dp')
- adapter_b_gradient: float32 [128, 5120], P(None, 'tensor')
- loss: float32 [], replicated
Inputs may be any that keep to these rules, and one draw needn't show every extreme that they name: `lengths`: in every group some rollout has length 256.
All inputs are finite; a program needn't handle non-finite values.
Results may differ from a plain program's by a relative error of at most 0.0067.
Values may be sent and summed in bfloat16 or wider, within the bound.
A program may use at most 64 MiB of HBM per device.

v0:
```python
import jax
import jax.numpy as jnp
from jax import lax
from jax.sharding import PartitionSpec as P

clip_eps = 0.2
adapter_scale_factor = 2.0


def token_terms(length_row, reward_row, log_ratio, offset):
    reward = reward_row.astype(jnp.float32)
    center = jnp.mean(reward)
    spread = jnp.mean((reward - center) * (reward - center))
    advantage = (reward - center) / jnp.sqrt(spread + 1.0)
    ends = jnp.cumsum(length_row)
    starts = ends - length_row
    slots = jnp.arange(log_ratio.shape[0], dtype=jnp.int32) + offset
    member = ((slots[None, :] >= starts[:, None]) & (slots[None, :] < ends[:, None])).astype(
        jnp.float32
    )
    live = jnp.sum(member, axis=0)
    token_adv = jnp.sum(member * advantage[:, None], axis=0)
    ratio = jnp.exp(log_ratio)
    unclipped = ratio * token_adv
    clipped = jnp.clip(ratio, 1.0 - clip_eps, 1.0 + clip_eps) * token_adv
    token_loss = -jnp.minimum(unclipped, clipped)
    slope = jnp.where(unclipped <= clipped, -unclipped, jnp.zeros_like(unclipped))
    return (live * slope, jnp.sum(live * token_loss), jnp.sum(live))


def local(activations, output_gradient, adapter_a, adapter_b, log_ratio, lengths, rewards):
    tokens = activations.shape[0]
    groups = lengths.shape[0]
    per_group = lax.axis_size("dp") // groups
    position = lax.axis_index("dp")
    group_id = position // per_group
    offset = position % per_group * tokens
    length_row = lax.dynamic_index_in_dim(lengths, group_id, 0, keepdims=False)
    reward_row = lax.dynamic_index_in_dim(rewards, group_id, 0, keepdims=False)
    token_coefficient, loss_local, live_count = token_terms(
        length_row, reward_row, log_ratio, offset
    )
    columns = activations
    partial_low = jnp.dot(
        columns,
        lax.all_gather(adapter_a, "dp", axis=1, tiled=True)[0],
        preferred_element_type=jnp.float32,
    )
    partial_back = lax.dot_general(
        output_gradient, adapter_b, (((1,), (1,)), ((), ())), preferred_element_type=jnp.float32
    )
    low_rank, backward_projection = lax.psum((partial_low, partial_back), "tensor")
    error_rows = (adapter_scale_factor * token_coefficient[:, None] * backward_projection).astype(
        jnp.bfloat16
    )
    weighted_error = token_coefficient[:, None] * low_rank
    local_adapter_b_gradient = adapter_scale_factor * jnp.einsum(
        "tr,td->rd",
        weighted_error,
        output_gradient.astype(jnp.float32),
        precision=lax.Precision.HIGHEST,
    )
    columns = activations
    grad_a = lax.psum_scatter(
        lax.dot_general(
            columns, error_rows, (((0,), (0,)), ((), ())), preferred_element_type=jnp.float32
        ),
        "dp",
        scatter_dimension=0,
        tiled=True,
    )
    grad_b_sum, loss_sum, live_sum = lax.psum(
        (local_adapter_b_gradient, loss_local, live_count), "dp"
    )
    factor = groups / live_sum
    return ((factor * grad_a)[None], factor * grad_b_sum, factor * loss_sum)


def solution(mesh):
    in_specs = (
        P("dp", "tensor"),
        P("dp", "tensor"),
        P("tensor", "dp", None),
        P(None, "tensor"),
        P("dp"),
        P(),
        P(),
    )
    out_specs = (P("tensor", "dp", None), P(None, "tensor"), P())
    return jax.shard_map(local, mesh=mesh, in_specs=in_specs, out_specs=out_specs, check_vma=False)
```

profile of v0, /device:TPU:0, one launch (start us, length us, event | category | flops | bytes accessed | tf_op | source)
XLA Modules:
  0.0 290.5 jit_solution(11864515134774246795)
XLA Ops:
  7.2 0.0 copy-start
  7.2 0.0 all-gather.2.cloned.1.call-start
  7.2 0.7 all-gather.2.cloned.1.call-update
  7.9 0.0 all-reduce.7.cloned.1.call-start
  8.0 1.3 convert_reduce_fusion.2
  9.9 1.3 multiply_reduce_fusion.1
  11.8 0.7 copy.16
  12.6 0.1 reduce.3
  12.7 0.7 divide_bitcast_fusion
  13.4 0.7 bitcast_subtract_fusion
  14.1 0.0 copy-done
  14.1 2.2 fusion.7
  16.3 0.0 copy-start.2
  16.3 43.8 %all-gather.2.cloned.1.call-done = bf16[1,13824,128]{2,1,0:T(8,128)(2,1)} async-done(((bf16[1,864,128]{2,1,0:T(8,128)(2,1)}), bf16[1,13824,128]{2,1,0:T(8,128)(2,1)}) %all-gather.2.cloned.1.call-update) | async-done | bytes 3538960 | tf_op jit(solution)/shard_map/all_gather | solution.py:46
  60.2 6.7 %fusion = f32[256,128]{1,0:T(8,128)} fusion(bf16[256,13824]{1,0:T(8,128)(2,1)} %param.7, bf16[1,13824,128]{2,1,0:T(8,128)(2,1)} %all-gather.2.cloned.1.call-done), kind=kOutput, calls=%fused_computation.2 | convolution fusion | flops 905969664 | bytes 10747904 | tf_op jit(solution)/shard_map/dot_general | solution.py:44
  66.8 0.0 all-reduce.7.cloned.1.call-update
  66.9 0.0 all-reduce.5.cloned.1.call-start
  66.9 0.7 convert_reduce_fusion.1
  67.6 0.0 copy-done.2
  67.6 0.6 broadcast_multiply_fusion.1
  68.2 20.8 %all-reduce.7.cloned.1.call-done = (f32[256,128]{1,0:T(8,128)}, f32[256,128]{1,0:T(8,128)}) async-done(((f32[256,128]{1,0:T(8,128)}, f32[256,128]{1,0:T(8,128)}), (f32[256,128]{1,0:T(8,128)}, f32[256,128]{1,0:T(8,128)})) %all-reduce.7.cloned.1.call-update) | async-done | bytes 262160 | tf_op jit(solution)/shard_map/psum | solution.py:52
  88.9 2.7 convolution_multiply_fusion
  91.7 0.0 copy-start.1
  91.7 0.0 all-reduce.5.cloned.1.call-update
  91.7 0.0 reduce-scatter.4.cloned.1.call-start
  91.8 0.8 copy-done.1
  92.6 7.2 %convolution_bitcast_fusion = f32[13824,128]{0,1:T(8,128)} fusion(bf16[256,13824]{1,0:T(8,128)(2,1)} %param.7, f32[256,128]{1,0:T(8,128)S(1)} %copy-done.1, f32[256]{0:T(256)S(1)} %get-tuple-element.22), kind=kOutput, calls=%fused_computation | convolution fusion | flops 906035200 | bytes 14287872 | tf_op jit(solution)/shard_map/dot_general | solution.py:65
  99.8 8.4 %copy.18 = f32[13824,128]{1,0:T(8,128)} copy(f32[13824,128]{0,1:T(8,128)} %convolution_bitcast_fusion) | data formatting | bytes 14155776
  108.2 0.0 reduce-scatter.4.cloned.1.call-update
  108.2 33.6 %all-reduce = (f32[]{:T(128)}, f32[]{:T(128)}) all-reduce(f32[]{:T(128)} %get-tuple-element.15, f32[]{:T(128)} %get-tuple-element.24), channel_id=1, replica_groups=mesh['dp'=16,'tensor'=2] {'dp'}, use_global_device_ids=true, to_apply=%region_2.3 | all-reduce | flops 2 | bytes 16 | tf_op jit(solution)/shard_map/psum | solution.py:72
  143.1 44.0 %all-reduce.5.cloned.1.call-done = f32[128,2560]{1,0:T(8,128)} async-done(((f32[128,2560]{1,0:T(8,128)}), f32[128,2560]{1,0:T(8,128)}) %all-reduce.5.cloned.1.call-update) | async-done | bytes 1310736 | tf_op jit(solution)/shard_map/psum | solution.py:72
  187.1 2.5 broadcast_multiply_fusion
  189.6 91.1 %reduce-scatter.4.cloned.1.call-done = f32[864,128]{1,0:T(8,128)} async-done(((f32[13824,128]{1,0:T(8,128)}), f32[864,128]{1,0:T(8,128)}) %reduce-scatter.4.cloned.1.call-update) | async-done | bytes 442384
  280.6 1.2 copy.19
  281.9 1.0 copy.17
  (3 shorter events, 0.1 us)
Async XLA Ops:
  7.2 6.9 %copy-start = (bf16[256,2560]{1,0:T(8,128)(2,1)S(1)}, bf16[256,2560]{1,0:T(8,128)(2,1)}, u32[]{:S(2)}) copy-start(bf16[256,2560]{1,0:T(8,128)(2,1)} %param.8) | copy-start | bytes 3932164
  7.2 53.0 %all-gather.2.cloned.1.call-start = ((), (), s32[]{:S(2)}) async-start(), calls=%async_computation.1 | async-start | bytes 3760128 | tf_op jit(solution)/shard_map/all_gather | solution.py:46
  7.9 81.0 %all-reduce.7.cloned.1.call-start = ((), (), s32[]{:S(2)}) async-start(), calls=%async_computation.4 | async-start | bytes 524288 | tf_op jit(solution)/shard_map/psum | solution.py:52
  16.3 51.3 %copy-start.2 = (f32[256]{0:T(256)S(1)}, f32[256]{0:T(256)}, u32[]{:S(2)}) copy-start(f32[256]{0:T(256)} %param.11) | copy-start | bytes 3076
  66.9 120.3 %all-reduce.5.cloned.1.call-start = ((), (), s32[]{:S(2)}) async-start(), calls=%async_computation.2 | async-start | bytes 2621440 | tf_op jit(solution)/shard_map/psum | solution.py:72
  91.7 0.9 copy-start.1
  91.7 188.9 %reduce-scatter.4.cloned.1.call-start = ((), (), s32[]{:S(2)}) async-start(), calls=%async_computation.3 | async-start | bytes 7520256
Sparse Core Ops, SparseCore 0:
  10.3 49.8 all-gather.1
  67.0 21.9 all-reduce.6
  93.0 94.0 all-reduce.4
  191.0 89.6 reduce-scatter.3
where the time goes:
time: 291 us
  waiting for transfers between devices  200 us (69%)
  blocking collectives  33.6 us (12%)
  matrix products  18.8 us (6%)
  between operations  17.6 us (6%)
  local copies, waits for them, and re-layouts  12.2 us (4%)
  other arithmetic  7.82 us (3%)
    unnamed x5, waiting for transfers between devices  91.8 us
    psum x1, waiting for transfers between devices, local(): lax.psum((local_adapter_b_gradient, loss_local, live_count), 'dp')  44 us
    all_gather x1, waiting for transfers between devices, local(): lax.all_gather(adapter_a, 'dp', axis=1, tiled=True)[0]  43.8 us
    psum x1, blocking collectives, local(): lax.psum((local_adapter_b_gradient, loss_local, live_count), 'dp')  33.6 us
    psum x1, waiting for transfers between devices, local(): lax.psum((partial_low, partial_back), 'tensor')  20.8 us
    unnamed x9, local copies, waits for them, and re-layouts  11.4 us
    dot_general x1, matrix products, local(): lax.dot_general(columns, error_rows, (((0,), (0,)), ((), ())), preferred_...  7.15 us
    dot_general x1, matrix products, local(): jnp.dot(columns, lax.all_gather(adapter_a, 'dp', axis=1, tiled=True)[0],...  6.66 us
  transfers between devices with their start and end apart: 4, of which 4 were waited for; matrix products, arithmetic and copies ran while one was open for 9% of the time, Pallas kernels for 0%

commit v1 on v0

--- a/solution.py
+++ b/solution.py
@@ -5,6 +5,13 @@
 
 clip_eps = 0.2
 adapter_scale_factor = 2.0
+
+
+def gather_over(block, mesh_axis, d):
+    devices = lax.axis_size(mesh_axis)
+    parts = jnp.stack([block for _ in range(devices)])
+    parts = lax.all_to_all(parts, mesh_axis, split_axis=0, concat_axis=0)
+    return jnp.concatenate(parts, axis=d)
 
 
 def token_terms(length_row, reward_row, log_ratio, offset):
@@ -42,9 +49,7 @@
     )
     columns = activations
     partial_low = jnp.dot(
-        columns,
-        lax.all_gather(adapter_a, "dp", axis=1, tiled=True)[0],
-        preferred_element_type=jnp.float32,
+        columns, gather_over(adapter_a, "dp", 1)[0], preferred_element_type=jnp.float32
     )
     partial_back = lax.dot_general(
         output_gradient, adapter_b, (((1,), (1,)), ((), ())), preferred_element_type=jnp.float32

time: 291 us -> 329 us (1.13)
  waiting for transfers between devices: 200 us -> 232 us
  starting transfers between devices: 0.16 us -> 7.72 us
    all_to_all x0 -> x1, waiting for transfers between devices: none -> 62.1 us  [gather_over(): parts = lax.all_to_all(parts, mesh_axis, split_axis=0, concat_axis=0)]
    all_gather x1 -> x0, waiting for transfers between devices: 43.8 us -> none  [local(): lax.all_gather(adapter_a, 'dp', axis=1, tiled=True)[0]]
    psum x1, waiting for transfers between devices: 20.8 us -> 34.6 us  [local(): lax.psum((partial_low, partial_back), 'tensor')]
    all_to_all x0 -> x1, starting transfers between devices: none -> 7.59 us  [gather_over(): parts = lax.all_to_all(parts, mesh_axis, split_axis=0, concat_axis=0)]
    unnamed x5 -> x4, waiting for transfers between devices: 91.8 us -> 91.2 us
    unnamed x9 -> x15, local copies, waits for them, and re-layouts: 11.4 us -> 11.5 us
  transfers between devices with their start and end apart: 4 -> 4, of which waited for: 4 -> 4; matrix products, arithmetic and copies ran while one was open for 9% -> 7% of each run, Pallas kernels for 0% -> 0%
where the time goes in v1:
time: 329 us; the launch traced here: 328 us
  waiting for transfers between devices  232 us (71%)
  blocking collectives  33.6 us (10%)
  matrix products  17.7 us (5%)
  between operations  17.7 us (5%)
  local copies, waits for them, and re-layouts  14.8 us (4%)
  starting transfers between devices  7.72 us (2%)
  other arithmetic  5.18 us (2%)
    unnamed x4, waiting for transfers between devices  91.2 us
    all_to_all x1, waiting for transfers between devices, gather_over(): parts = lax.all_to_all(parts, mesh_axis, split_axis=0, concat_axis=0)  62.1 us
    psum x1, waiting for transfers between devices, local(): lax.psum((local_adapter_b_gradient, loss_local, live_count), 'dp')  43.9 us
    psum x1, waiting for transfers between devices, local(): lax.psum((partial_low, partial_back), 'tensor')  34.6 us
    psum x1, blocking collectives, local(): lax.psum((local_adapter_b_gradient, loss_local, live_count), 'dp')  33.6 us
    unnamed x15, local copies, waits for them, and re-layouts  11.5 us
    all_to_all x1, starting transfers between devices, gather_over(): parts = lax.all_to_all(parts, mesh_axis, split_axis=0, concat_axis=0)  7.59 us
    dot_general x1, matrix products, local(): lax.dot_general(columns, error_rows, (((0,), (0,)), ((), ())), preferred_...  7.15 us
  transfers between devices with their start and end apart: 4, of which 4 were waited for; matrix products, arithmetic and copies ran while one was open for 7% of the time, Pallas kernels for 0%

profile of v1, /device:TPU:0, one launch (start us, length us, event | category | flops | bytes accessed | tf_op | source)
XLA Modules:
  0.0 328.5 jit_solution(12532151226707070565)
XLA Ops:
  7.2 0.0 copy-start
  7.2 3.3 %stack.2 = bf16[16,1,864,128]{3,2,1,0:T(8,128)(2,1)} broadcast(bf16[864,128]{1,0:T(8,128)(2,1)} %bitcast.18), dimensions={2,3} | broadcast | bytes 3760128 | tf_op jit(solution)/shard_map/stack | solution.py:12
  10.5 0.0 copy-start.5
  10.5 0.0 copy-start.4
  10.5 0.0 copy-start.1
  10.5 7.6 %all-to-all-start = ((bf16[16,1,864,128]{3,2,1,0:T(8,128)(2,1)}), bf16[16,1,864,128]{3,2,1,0:T(8,128)(2,1)}, u32[]{:S(2)}, u32[]{:S(2)}) async-start(bf16[16,1,864,128]{3,2,1,0:T(8,128)(2,1)} %stack.2), calls=%async_computation | async-start | bytes 7077888 | tf_op jit(solution)/shard_map/all_to_all | solution.py:13
  18.1 0.0 all-reduce.7.cloned.1.call-start
  18.1 0.0 copy-done.5
  18.2 0.6 convert_reduce_fusion.2
  19.4 0.6 multiply_reduce_fusion.1
  20.7 0.0 copy-done.4
  20.7 0.1 copy.16
  20.8 0.1 reduce.3
  21.0 0.0 copy-done
  21.0 0.0 copy-done.1
  21.0 1.2 fusion.5
  22.2 62.1 %all-to-all-done = bf16[16,1,864,128]{3,2,1,0:T(8,128)(2,1)} async-done(((bf16[16,1,864,128]{3,2,1,0:T(8,128)(2,1)}), bf16[16,1,864,128]{3,2,1,0:T(8,128)(2,1)}, u32[]{:S(2)}, u32[]{:S(2)}) %all-to-all-start) | async-done | bytes 3538976 | tf_op jit(solution)/shard_map/all_to_all | solution.py:13
  84.2 0.0 copy-start.3
  84.2 6.7 %fusion.6 = f32[256,128]{1,0:T(8,128)} fusion(bf16[256,13824]{1,0:T(8,128)(2,1)} %param.7, bf16[13824,128]{1,0:T(8,128)(2,1)} %bitcast.6), kind=kOutput, calls=%fused_computation.25 | convolution fusion | flops 905969664 | bytes 10747904 | tf_op jit(solution)/shard_map/dot_general | solution.py:51
  90.9 0.0 all-reduce.7.cloned.1.call-update
  90.9 0.0 all-reduce.5.cloned.1.call-start
  91.0 0.7 convert_reduce_fusion.1
  91.7 0.0 copy-done.3
  91.7 0.6 broadcast_multiply_fusion.1
  92.3 34.6 %all-reduce.7.cloned.1.call-done = (f32[256,128]{1,0:T(8,128)}, f32[256,128]{1,0:T(8,128)}) async-done(((f32[256,128]{1,0:T(8,128)}, f32[256,128]{1,0:T(8,128)}), (f32[256,128]{1,0:T(8,128)}, f32[256,128]{1,0:T(8,128)})) %all-reduce.7.cloned.1.call-update) | async-done | bytes 262160 | tf_op jit(solution)/shard_map/psum | solution.py:57
  126.8 2.7 convolution_multiply_fusion
  129.6 0.0 copy-start.2
  129.6 0.0 all-reduce.5.cloned.1.call-update
  129.6 0.0 reduce-scatter.4.cloned.1.call-start
  129.7 0.8 copy-done.2
  130.5 7.1 %convolution_bitcast_fusion = f32[13824,128]{0,1:T(8,128)} fusion(bf16[256,13824]{1,0:T(8,128)(2,1)} %param.7, f32[256,128]{1,0:T(8,128)S(1)} %copy-done.2, f32[256]{0:T(256)S(1)} %get-tuple-element.22), kind=kOutput, calls=%fused_computation | convolution fusion | flops 906035200 | bytes 14287872 | tf_op jit(solution)/shard_map/dot_general | solution.py:70
  137.6 8.4 %copy.18 = f32[13824,128]{1,0:T(8,128)} copy(f32[13824,128]{0,1:T(8,128)} %convolution_bitcast_fusion) | data formatting | bytes 14155776
  146.1 0.0 reduce-scatter.4.cloned.1.call-update
  146.1 33.6 %all-reduce = (f32[]{:T(128)}, f32[]{:T(128)}) all-reduce(f32[]{:T(128)} %get-tuple-element.15, f32[]{:T(128)} %get-tuple-element.24), channel_id=1, replica_groups=mesh['dp'=16,'tensor'=2] {'dp'}, use_global_device_ids=true, to_apply=%region_2.3 | all-reduce | flops 2 | bytes 16 | tf_op jit(solution)/shard_map/psum | solution.py:77
  181.0 43.9 %all-reduce.5.cloned.1.call-done = f32[128,2560]{1,0:T(8,128)} async-done(((f32[128,2560]{1,0:T(8,128)}), f32[128,2560]{1,0:T(8,128)}) %all-reduce.5.cloned.1.call-update) | async-done | bytes 1310736 | tf_op jit(solution)/shard_map/psum | solution.py:77
  224.9 2.5 broadcast_multiply_fusion
  227.4 91.2 %reduce-scatter.4.cloned.1.call-done = f32[864,128]{1,0:T(8,128)} async-done(((f32[13824,128]{1,0:T(8,128)}), f32[864,128]{1,0:T(8,128)}) %reduce-scatter.4.cloned.1.call-update) | async-done | bytes 442384
  318.6 1.2 copy.19
  319.9 1.0 copy.17
  (5 shorter events, 0.1 us)
Async XLA Ops:
  7.2 13.8 %copy-start = (bf16[256,2560]{1,0:T(8,128)(2,1)S(1)}, bf16[256,2560]{1,0:T(8,128)(2,1)}, u32[]{:S(2)}) copy-start(bf16[256,2560]{1,0:T(8,128)(2,1)} %param.8) | copy-start | bytes 3932164
  10.5 7.7 %copy-start.5 = (s32[1,16]{1,0:T(1,128)S(1)}, s32[1,16]{1,0:T(1,128)}, u32[]{:S(2)}) copy-start(s32[1,16]{1,0:T(1,128)} %param.13) | copy-start | bytes 196
  10.5 10.2 %copy-start.4 = (s32[1,16]{1,0:T(1,128)S(1)}, s32[1,16]{1,0:T(1,128)}, u32[]{:S(2)}) copy-start(s32[1,16]{1,0:T(1,128)} %param.12) | copy-start | bytes 196
  10.5 10.5 %copy-start.1 = (bf16[128,2560]{1,0:T(8,128)(2,1)S(1)}, bf16[128,2560]{1,0:T(8,128)(2,1)}, u32[]{:S(2)}) copy-start(bf16[128,2560]{1,0:T(8,128)(2,1)} %param.10) | copy-start | bytes 1966084
  10.5 73.7 %all-to-all-start = ((bf16[16,1,864,128]{3,2,1,0:T(8,128)(2,1)}), bf16[16,1,864,128]{3,2,1,0:T(8,128)(2,1)}, u32[]{:S(2)}, u32[]{:S(2)}) async-start(bf16[16,1,864,128]{3,2,1,0:T(8,128)(2,1)} %stack.2), calls=%async_computation | async-start | bytes 7077888 | tf_op jit(solution)/shard_map/all_to_all | solution.py:13
  18.1 108.7 %all-reduce.7.cloned.1.call-start = ((), (), s32[]{:S(2)}) async-start(), calls=%async_computation.4 | async-start | bytes 524288 | tf_op jit(solution)/shard_map/psum | solution.py:57
  84.2 7.4 %copy-start.3 = (f32[256]{0:T(256)S(1)}, f32[256]{0:T(256)}, u32[]{:S(2)}) copy-start(f32[256]{0:T(256)} %param.11) | copy-start | bytes 3076
  90.9 134.0 %all-reduce.5.cloned.1.call-start = ((), (), s32[]{:S(2)}) async-start(), calls=%async_computation.2 | async-start | bytes 2621440 | tf_op jit(solution)/shard_map/psum | solution.py:77
  129.6 0.9 copy-start.2
  129.6 189.0 %reduce-scatter.4.cloned.1.call-start = ((), (), s32[]{:S(2)}) async-start(), calls=%async_computation.3 | async-start | bytes 7520256
Sparse Core Ops, SparseCore 0:
  91.0 35.7 all-reduce.6
  130.9 94.0 all-reduce.4
  229.0 89.6 reduce-scatter.3
